TPU v7x, 32 devices: a whole 2x2x4 slice. The times are simulated.
32 devices in a mesh: row: 16 (over z, y, core), col: 2 (over x).
Axes of the slice: x: 2, y: 2, z: 4, core: 2. Of those that a mesh axis runs over, the one named last changes fastest.
Arguments:
- left: bfloat16 [16384, 16384], P('row', 'col'), may hold values from -6 to 6
- right: bfloat16 [16384, 16384], P('row', 'col'), may hold values from -0.09375 to 0.09375
Outputs:
- product: bfloat16 [16384, 16384], P('row', 'col')
All inputs are finite; a program needn't handle non-finite values.
Results may differ from a plain program's by a relative error of at most 0.001.
Values may be sent and summed in bfloat16 or wider, within the bound.
A program may use at most 256 MiB of HBM per device.

v0:
```python
import jax
import jax.numpy as jnp
from jax import lax
from jax.sharding import PartitionSpec as P

STEPS = 4


def broadcast(value, axis, source):
    kept = jnp.where(lax.axis_index(axis) == source, value, 0).astype(value.dtype)
    return lax.psum(kept, axis)


def from_behind(block, axis, distance):
    devices = range(lax.axis_size(axis))
    route = [((i - distance) % len(devices), i) for i in devices]
    return lax.ppermute(block, axis, route)


def local(left, right):
    grid_rows = lax.axis_size("row")
    col_count = lax.axis_size("col")
    block_rows = left.shape[0]
    per_shard = grid_rows // col_count
    row_index = lax.axis_index("row")
    partial_sum = jnp.zeros((block_rows, right.shape[1]), jnp.float32)
    right_rows = right
    for offset in range(STEPS):
        kblock = (row_index + offset) % grid_rows
        left_piece = lax.dynamic_slice_in_dim(left, kblock % per_shard * block_rows, block_rows, 1)
        left_block = broadcast(left_piece, "col", kblock // per_shard)
        if offset > 0:
            right_rows = from_behind(right_rows, "row", -1)
        partial_sum = partial_sum + jnp.dot(
            left_block, right_rows, preferred_element_type=jnp.float32
        )
    return partial_sum.astype(jnp.bfloat16)


def solution(mesh):
    return jax.shard_map(
        local,
        mesh=mesh,
        in_specs=(P("row", "col"), P("row", "col")),
        out_specs=P("row", "col"),
        check_vma=False,
    )
```

profile of v0, /device:TPU:0, one launch (start us, length us, event | category | flops | bytes accessed | tf_op | source)
XLA Modules:
  0.0 617.2 jit_solution(10150321549092427315)
XLA Ops:
  6.5 0.0 all-reduce.3.cloned.1.call-start
  6.5 5.5 collective-permute-start
  12.0 181.2 %collective-permute-done = bf16[1024,8192]{1,0:T(8,128)(2,1)} collective-permute-done((bf16[1024,8192]{1,0:T(8,128)(2,1)}, bf16[1024,8192]{1,0:T(8,128)(2,1)}, u32[]{:S(2)}, u32[]{:S(2)}) %collective-permute-start) | collective-permute-done | bytes 16777248 | tf_op jit(solution)/shard_map/ppermute | solution.py:17
  193.2 4.6 collective-permute-start.1
  197.8 8.6 %dynamic-slice_select_fusion = (bf16[1024,1024]{1,0:T(8,128)(2,1)}, bf16[1024,1024]{1,0:T(8,128)(2,1)}, bf16[1024,1024]{1,0:T(8,128)(2,1)}, bf16[1024,1024]{1,0:T(8,128)(2,1)}) fusion(bf16[1024,8192]{1,0:T(8,128)(2,1)} %param.2, s32[]{:T(128)S(6)} %select_n.108, pred[]{:T(512)S(6)} %eq.24, s32[]{:T(128)S(6)} %select_n.96, pred[]{:T(512)S(6)} %eq.22, ...), kind=kLoop, calls=%fused_computation.1 | loop fusion | flops 4194304 | bytes 16777236 | tf_op jit(solution)/shard_map/jit(_where)/select_n | solution.py:10
  206.4 0.0 all-reduce.3.cloned.1.call-update
  206.4 172.5 %collective-permute-done.1 = bf16[1024,8192]{1,0:T(8,128)(2,1)} collective-permute-done((bf16[1024,8192]{1,0:T(8,128)(2,1)}, bf16[1024,8192]{1,0:T(8,128)(2,1)}, u32[]{:S(2)}, u32[]{:S(2)}) %collective-permute-start.1) | collective-permute-done | bytes 16777248 | tf_op jit(solution)/shard_map/ppermute | solution.py:17
  378.9 4.6 collective-permute-start.2
  383.5 18.4 %all-reduce.3.cloned.1.call-done = (bf16[1024,1024]{1,0:T(8,128)(2,1)}, bf16[1024,1024]{1,0:T(8,128)(2,1)}, bf16[1024,1024]{1,0:T(8,128)(2,1)}, bf16[1024,1024]{1,0:T(8,128)(2,1)}) async-done(((bf16[1024,1024]{1,0:T(8,128)(2,1)}, bf16[1024,1024]{1,0:T(8,128)(2,1)}, bf16[1024,1024]{1,0:T(8,128)(2,1)}, bf16[1024,1024]{1,0:T(8,128)(2,1)}), (bf16[1024,1024]{1,0:T(8,128)(2,1)}, bf16[1024,1024]{1,0:T(8,128)(2,1)}, ...) | async-done | bytes 8388624 | tf_op jit(solution)/shard_map/psum | solution.py:11
  401.9 0.0 copy-start.1
  401.9 27.5 %fusion = f32[1024,8192]{1,0:T(8,128)} fusion(bf16[1024,1024]{1,0:T(8,128)(2,1)} %get-tuple-element.6, bf16[1024,8192]{1,0:T(8,128)(2,1)} %param.3), kind=kOutput, calls=%fused_computation.5 | convolution fusion | flops 17179869184 | bytes 52428800 | tf_op jit(solution)/shard_map/dot_general | solution.py:34
  429.5 0.0 copy-done.1
  429.5 26.7 %fusion.1 = f32[1024,8192]{1,0:T(8,128)} fusion(bf16[1024,1024]{1,0:T(8,128)(2,1)S(1)} %copy-done.1, bf16[1024,8192]{1,0:T(8,128)(2,1)} %collective-permute-done), kind=kOutput, calls=%fused_computation.6 | convolution fusion | flops 17179869184 | bytes 52428800 | tf_op jit(solution)/shard_map/dot_general | solution.py:34
  456.2 0.0 copy-start
  456.2 27.6 %fusion.2 = f32[1024,8192]{1,0:T(8,128)} fusion(bf16[1024,1024]{1,0:T(8,128)(2,1)} %get-tuple-element.5, bf16[1024,8192]{1,0:T(8,128)(2,1)} %collective-permute-done.1), kind=kOutput, calls=%fused_computation.7 | convolution fusion | flops 17179869184 | bytes 52428800 | tf_op jit(solution)/shard_map/dot_general | solution.py:34
  483.8 80.9 %collective-permute-done.2 = bf16[1024,8192]{1,0:T(8,128)(2,1)} collective-permute-done((bf16[1024,8192]{1,0:T(8,128)(2,1)}, bf16[1024,8192]{1,0:T(8,128)(2,1)}, u32[]{:S(2)}, u32[]{:S(2)}) %collective-permute-start.2) | collective-permute-done | bytes 16777248 | tf_op jit(solution)/shard_map/ppermute | solution.py:17
  564.7 0.0 copy-done
  564.7 45.6 %add_convert_fusion = bf16[1024,8192]{1,0:T(8,128)(2,1)} fusion(f32[1024,8192]{1,0:T(8,128)} %fusion.2, f32[1024,8192]{1,0:T(8,128)} %fusion, f32[1024,8192]{1,0:T(8,128)} %fusion.1, bf16[1024,1024]{1,0:T(8,128)(2,1)S(1)} %copy-done, bf16[1024,8192]{1,0:T(8,128)(2,1)} %collective-permute-done.2), kind=kOutput, calls=%fused_computation | convolution fusion | flops 17213423616 | bytes 136314880 | tf_op jit(solution)/shard_map/dot_general | solution.py:34
Async XLA Ops:
  6.5 395.4 %all-reduce.3.cloned.1.call-start = ((), (), s32[]{:S(2)}) async-start(), calls=%async_computation | async-start | bytes 16777216 | tf_op jit(solution)/shard_map/psum | solution.py:11
  6.5 186.6 %collective-permute-start = (bf16[1024,8192]{1,0:T(8,128)(2,1)}, bf16[1024,8192]{1,0:T(8,128)(2,1)}, u32[]{:S(2)}, u32[]{:S(2)}) collective-permute-start(bf16[1024,8192]{1,0:T(8,128)(2,1)} %param.3), channel_id=1, source_target_pairs={{2,0},{4,2},{6,4},{8,6},{10,8},{12,10},{14,12},{16,14},{18,16},{20... | collective-permute-start | bytes 50331656 | tf_op jit(solution)/shard_map/ppermute | solution.py:17
  193.2 185.8 %collective-permute-start.1 = (bf16[1024,8192]{1,0:T(8,128)(2,1)}, bf16[1024,8192]{1,0:T(8,128)(2,1)}, u32[]{:S(2)}, u32[]{:S(2)}) collective-permute-start(bf16[1024,8192]{1,0:T(8,128)(2,1)} %collective-permute-done), channel_id=1, source_target_pairs={{2,0},{4,2},{6,4},{8,6},{10,8},{12,10},{14,12},{16,14},{18,16},{20... | collective-permute-start | bytes 50331656 | tf_op jit(solution)/shard_map/ppermute | solution.py:17
  378.9 185.8 %collective-permute-start.2 = (bf16[1024,8192]{1,0:T(8,128)(2,1)}, bf16[1024,8192]{1,0:T(8,128)(2,1)}, u32[]{:S(2)}, u32[]{:S(2)}) collective-permute-start(bf16[1024,8192]{1,0:T(8,128)(2,1)} %collective-permute-done.1), channel_id=1, source_target_pairs={{2,0},{4,2},{6,4},{8,6},{10,8},{12,10},{14,12},{16,14},{18,16},{20... | collective-permute-start | bytes 50331656 | tf_op jit(solution)/shard_map/ppermute | solution.py:17
  401.9 27.5 %copy-start.1 = (bf16[1024,1024]{1,0:T(8,128)(2,1)S(1)}, bf16[1024,1024]{1,0:T(8,128)(2,1)}, u32[]{:S(2)}) copy-start(bf16[1024,1024]{1,0:T(8,128)(2,1)} %get-tuple-element.7) | copy-start | bytes 6291460
  456.2 108.5 %copy-start = (bf16[1024,1024]{1,0:T(8,128)(2,1)S(1)}, bf16[1024,1024]{1,0:T(8,128)(2,1)}, u32[]{:S(2)}) copy-start(bf16[1024,1024]{1,0:T(8,128)(2,1)} %get-tuple-element.8) | copy-start | bytes 6291460
Sparse Core Ops, SparseCore 0:
  206.6 195.3 all-reduce.2
where the time goes:
time: 617 us
  waiting for transfers between devices  453 us (73%)
  matrix products  128 us (21%)
  starting transfers between devices  14.7 us (2%)
  between operations  13.4 us (2%)
  other arithmetic  8.63 us (1%)
    ppermute x3, waiting for transfers between devices, from_behind(): return lax.ppermute(block, axis, route)  435 us
    dot_general x4, matrix products, local(): jnp.dot(left_block, right_rows, preferred_element_type=jnp.float32)  128 us
    psum x1, waiting for transfers between devices, broadcast(): return lax.psum(kept, axis)  18.4 us
    ppermute x3, starting transfers between devices, from_behind(): return lax.ppermute(block, axis, route)  14.7 us
  transfers between devices with their start and end apart: 4, of which 4 were waited for; matrix products, arithmetic and copies ran while one was open for 15% of the time, Pallas kernels for 0%

commit v1 on v0

v1 whole, which is shorter than its diff:
```python
import functools

import jax
import jax.numpy as jnp
from jax import lax
from jax.experimental import pallas as pl
from jax.experimental.pallas import tpu as pltpu
from jax.sharding import PartitionSpec as P

STEPS = 4
WIDTH = 256
AHEAD = 6
BURST = 3
MESH = pl.DeviceIdType.MESH


def kernel(grid_rows, col_count, width, start, left, right, out, arr_a, arr_b, arr_z, arr_d,
           lbuf, rbuf, obuf, sem_a, sem_b, sem_z, sem_d, send, lsend, lrecv, load_sem, out_sem):
    row = lax.axis_index("row")
    col = lax.axis_index("col")
    rows, columns = right.shape
    chunks = columns // width
    per_shard = grid_rows // col_count
    c = row % 2
    p = (row // 2) % 2
    group = row - 2 * p - c
    partner = group + 2 * p + 1 - c
    across = group + 2 * (1 - p) + c
    z_to = (row + grid_rows - 3 - 2 * c) % grid_rows
    z_from = (row + 5 - 2 * c) % grid_rows

    barrier = pltpu.get_barrier_semaphore()
    for other in (partner, across, z_to, z_from):
        pl.semaphore_signal(barrier, inc=1, device_id={"row": other}, device_id_type=MESH)
    for step in range(1, col_count):
        pl.semaphore_signal(barrier, inc=1, device_id={"col": (col + step) % col_count}, device_id_type=MESH)
    pl.semaphore_wait(barrier, 4 + col_count - 1)

    def cut(ref, j):
        return ref.at[:, pl.ds(pl.multiple_of(j * width, width), width)]

    def remote(src, dst, j, which, recv, to):
        return pltpu.make_async_remote_copy(
            src_ref=cut(src, j), dst_ref=cut(dst, j), send_sem=send.at[which],
            recv_sem=recv.at[j], device_id={"row": to}, device_id_type=MESH)

    def arrival(dst, recv, j):
        pltpu.make_async_copy(cut(dst, j), cut(dst, j), recv.at[j]).wait()

    has_z_out = (p * c) == 0
    has_z_in = ((1 - p) + c) > 0

    def send_own(j):
        @pl.when(p == 1)
        def _():
            remote(right, arr_a, j, 0, sem_a, across).start()

        @pl.when(has_z_out)
        def _():
            remote(right, arr_z, j, 1, sem_z, z_to).start()

        @pl.when(c == 1)
        def _():
            remote(right, arr_d, j, 2, sem_d, partner).start()

    turns = (0, 2 + p * (1 - 2 * c), 2 + (1 - p) * (1 - 2 * c), 1 + 2 * c)

    def left_of(t):
        block = (row + turns[t]) % grid_rows
        source = left.at[:, pl.ds(pl.multiple_of(block % per_shard * rows, rows), rows)]
        slot = lbuf.at[:, pl.ds(t * rows, rows)]
        return block // per_shard, source, slot

    def left_copy(t, step):
        _, source, slot = left_of(t)
        return pltpu.make_async_remote_copy(
            src_ref=source, dst_ref=slot, send_sem=lsend.at[t, step - 1], recv_sem=lrecv.at[t],
            device_id={"col": (col + step) % col_count}, device_id_type=MESH)

    ahead = min(AHEAD, chunks)

    def first(j, _):
        send_own(j)
        return 0

    lax.fori_loop(0, ahead, first, 0)
    for t in range(STEPS):
        owner, source, slot = left_of(t)

        @pl.when(owner == col)
        def _():
            for step in range(1, col_count):
                left_copy(t, step).start()
            pltpu.make_async_copy(source, slot, lrecv.at[t]).start()

    def relay(i):
        @pl.when(i + ahead < chunks)
        def _():
            send_own(i + ahead)

        @pl.when(has_z_in)
        def _():
            arrival(arr_z, sem_z, i)

            @pl.when(p == 0)
            def _():
                remote(arr_z, arr_a, i, 4, sem_a, across).start()

        arrival(arr_a, sem_a, i)
        remote(arr_a, arr_b, i, 3, sem_b, partner).start()

    def load(src, j, slot, t):
        return pltpu.make_async_copy(
            cut(src, j), rbuf.at[slot, pl.ds(t * rows, rows), :], load_sem.at[slot, t])

    def store(j, slot):
        return pltpu.make_async_copy(obuf.at[slot], cut(out, j), out_sem.at[slot])

    def compute(first_chunk, count):
        for n in range(count):
            j = first_chunk + n
            arrival(arr_b, sem_b, j)
            load(right, j, n, 0).start()
            load(arr_a, j, n, 1).start()
            load(arr_b, j, n, 2).start()

            @pl.when(c == 0)
            def _():
                arrival(arr_d, sem_d, j)
                load(arr_d, j, n, 3).start()

            @pl.when(c == 1)
            def _():
                load(arr_z, j, n, 3).start()

        def one(n, _):
            for t in range(STEPS):
                load(right, first_chunk + n, n, t).wait()
            obuf[n] = jnp.dot(lbuf[...], rbuf[n], preferred_element_type=jnp.float32).astype(obuf.dtype)
            store(first_chunk + n, n).start()
            return 0

        lax.fori_loop(0, count, one, 0)
        for n in range(count):
            store(first_chunk + n, n).wait()

    def only_relay(i, _):
        relay(i)
        return 0

    lax.fori_loop(0, start, only_relay, 0)
    for t in range(STEPS):
        pltpu.make_async_copy(left_of(t)[2], left_of(t)[2], lrecv.at[t]).wait()

    def burst(i, _):
        relay(i)
        compute((i - start) * BURST, BURST)
        return 0

    caught = start + start // (BURST - 1)
    lax.fori_loop(start, caught, burst, 0)

    def level(i, _):
        relay(i)
        compute(i, 1)
        return 0

    lax.fori_loop(caught, chunks, level, 0)

    def sent(which):
        pltpu.make_async_copy(right, right, send.at[which]).wait()

    @pl.when(p == 1)
    def _():
        sent(0)

    @pl.when(has_z_out)
    def _():
        sent(1)

    @pl.when(c == 1)
    def _():
        sent(2)

    sent(3)

    @pl.when(p == 0)
    def _():
        sent(4)

    for t in range(STEPS):
        @pl.when(left_of(t)[0] == col)
        def _():
            for step in range(1, col_count):
                left_copy(t, step).wait_send()


def solution(mesh):
    grid_rows, col_count = mesh.shape["row"], mesh.shape["col"]

    def local(left, right):
        rows, columns = right.shape
        width = min(WIDTH, columns // 8)
        chunks = columns // width
        start = (chunks * 9 // 16) // 2 * 2
        block = jax.ShapeDtypeStruct((rows, columns), jnp.bfloat16)
        dma = pltpu.SemaphoreType.DMA
        results = pl.pallas_call(
            functools.partial(kernel, grid_rows, col_count, width, start),
            out_shape=[block] * 5,
            in_specs=[pl.BlockSpec(memory_space=pl.ANY)] * 2,
            out_specs=[pl.BlockSpec(memory_space=pl.ANY)] * 5,
            scratch_shapes=[
                pltpu.VMEM((rows, STEPS * rows), jnp.bfloat16),
                pltpu.VMEM((BURST, STEPS * rows, width), jnp.bfloat16),
                pltpu.VMEM((BURST, rows, width), jnp.bfloat16),
                dma((chunks,)), dma((chunks,)), dma((chunks,)), dma((chunks,)),
                dma((5,)), dma((STEPS, col_count - 1)), dma((STEPS,)),
                dma((BURST, STEPS)), dma((BURST,)),
            ],
            compiler_params=pltpu.CompilerParams(
                collective_id=0, has_side_effects=True, vmem_limit_bytes=60 * 1024 * 1024),
        )(left, right)
        return results[0]

    return jax.shard_map(
        local,
        mesh=mesh,
        in_specs=(P("row", "col"), P("row", "col")),
        out_specs=P("row", "col"),
        check_vma=False,
    )
```

time: 617 us -> 401 us (0.65); the launches traced: 617 us -> 394 us
  waiting for transfers between devices: 453 us -> 0 us
  Pallas kernels: 0 us -> 380 us
  matrix products: 128 us -> 0 us
  starting transfers between devices: 14.7 us -> 0 us
  local copies, waits for them, and re-layouts: 0.01 us -> 14 us
  between operations: 13.4 us -> 0.01 us
  other arithmetic: 8.63 us -> 0 us
    ppermute x3 -> x0, waiting for transfers between devices: 435 us -> none  [from_behind(): return lax.ppermute(block, axis, route)]
    pallas_call x0 -> x1, Pallas kernels: none -> 380 us  [local(): pl.pallas_call(functools.partial(kernel, grid_rows, col_count, width, sta...]
    dot_general x4 -> x0, matrix products: 128 us -> none  [local(): jnp.dot(left_block, right_rows, preferred_element_type=jnp.float32)]
    psum x1 -> x0, waiting for transfers between devices: 18.4 us -> none  [broadcast(): return lax.psum(kept, axis)]
    ppermute x3 -> x0, starting transfers between devices: 14.7 us -> none  [from_behind(): return lax.ppermute(block, axis, route)]
    unnamed x4 -> x1, local copies, waits for them, and re-layouts: 0.01 us -> 14 us
    select_n x1 -> x0, other arithmetic: 8.63 us -> none  [broadcast(): jnp.where(lax.axis_index(axis) == source, value, 0).astype(value.dtype)]
  transfers between devices with their start and end apart: 4 -> 0, of which waited for: 4 -> 0; matrix products, arithmetic and copies ran while one was open for 15% -> 0% of each run, Pallas kernels for 0% -> 0%
where the time goes in v1:
time: 401 us; the launch traced here: 394 us
  Pallas kernels  380 us (95%)
  local copies, waits for them, and re-layouts  14 us (3%)
    pallas_call x1, Pallas kernels, local(): pl.pallas_call(functools.partial(kernel, grid_rows, col_count, width, sta...  380 us
    unnamed x1, local copies, waits for them, and re-layouts  14 us

profile of v1, /device:TPU:0, one launch (start us, length us, event | category | flops | bytes accessed | tf_op | source)
XLA Modules:
  0.0 393.6 jit_solution(2215180046439187025)
XLA Ops:
  0.0 379.6 %shard_map.28 = (bf16[1024,8192]{1,0:T(8,128)(2,1)}, bf16[1024,8192]{1,0:T(8,128)(2,1)}, bf16[1024,8192]{1,0:T(8,128)(2,1)}, bf16[1024,8192]{1,0:T(8,128)(2,1)}, bf16[1024,8192]{1,0:T(8,128)(2,1)}) custom-call(bf16[1024,8192]{1,0:T(8,128)(2,1)} %left.1, bf16[1024,8192]{1,0:T(8,128)(2,1)} %right.1), custom_call_target="tpu_custom_call" | custom-call | tf_op jit(solution)/shard_map/pallas_call | solution.py:208
  379.6 14.0 %copy.4 = bf16[1024,8192]{1,0:T(8,128)(2,1)} copy(bf16[1024,8192]{1,0:T(8,128)(2,1)} %get-tuple-element.6) | data formatting | bytes 33554432

commit v2 on v1

--- a/solution.py
+++ b/solution.py
@@ -11,11 +11,12 @@
 WIDTH = 256
 AHEAD = 6
 BURST = 3
+EARLY = 3
 MESH = pl.DeviceIdType.MESH
 
 
 def kernel(grid_rows, col_count, width, start, left, right, out, arr_a, arr_b, arr_z, arr_d,
-           lbuf, rbuf, obuf, sem_a, sem_b, sem_z, sem_d, send, lsend, lrecv, load_sem, out_sem):
+           lbuf, rbuf, sem_a, sem_b, sem_z, sem_d, send, lsend, lrecv, load_sem):
     row = lax.axis_index("row")
     col = lax.axis_index("col")
     rows, columns = right.shape
@@ -50,12 +51,19 @@
     has_z_out = (p * c) == 0
     has_z_in = ((1 - p) + c) > 0
 
+    odd_low = (1 - p) * c == 1
+    odd_high = p * c == 1
+
     def send_own(j):
+        @pl.when(odd_low & (j < EARLY))
+        def _():
+            remote(right, arr_d, j, 5, sem_d, across).start()
+
         @pl.when(p == 1)
         def _():
             remote(right, arr_a, j, 0, sem_a, across).start()
 
-        @pl.when(has_z_out)
+        @pl.when(has_z_out & ((c == 0) | (j >= EARLY)))
         def _():
             remote(right, arr_z, j, 1, sem_z, z_to).start()
 
@@ -98,7 +106,12 @@
         def _():
             send_own(i + ahead)
 
-        @pl.when(has_z_in)
+        @pl.when(odd_high & (i < EARLY))
+        def _():
+            arrival(arr_d, sem_d, i)
+            remote(arr_d, arr_a, i, 6, sem_a, z_to).start()
+
+        @pl.when(has_z_in & ((c == 1) | (i >= EARLY)))
         def _():
             arrival(arr_z, sem_z, i)
 
@@ -112,9 +125,6 @@
     def load(src, j, slot, t):
         return pltpu.make_async_copy(
             cut(src, j), rbuf.at[slot, pl.ds(t * rows, rows), :], load_sem.at[slot, t])
-
-    def store(j, slot):
-        return pltpu.make_async_copy(obuf.at[slot], cut(out, j), out_sem.at[slot])
 
     def compute(first_chunk, count):
         for n in range(count):
@@ -136,13 +146,11 @@
         def one(n, _):
             for t in range(STEPS):
                 load(right, first_chunk + n, n, t).wait()
-            obuf[n] = jnp.dot(lbuf[...], rbuf[n], preferred_element_type=jnp.float32).astype(obuf.dtype)
-            store(first_chunk + n, n).start()
+            out[first_chunk + n] = jnp.dot(
+                lbuf[...], rbuf[n], preferred_element_type=jnp.float32).astype(out.dtype)
             return 0
 
         lax.fori_loop(0, count, one, 0)
-        for n in range(count):
-            store(first_chunk + n, n).wait()
 
     def only_relay(i, _):
         relay(i)
@@ -167,24 +175,38 @@
 
     lax.fori_loop(caught, chunks, level, 0)
 
-    def sent(which):
-        pltpu.make_async_copy(right, right, send.at[which]).wait()
+    def sent(which, begin=0, end=chunks):
+        part = right.at[:, pl.ds(begin * width, (end - begin) * width)]
+        pltpu.make_async_copy(part, part, send.at[which]).wait()
 
     @pl.when(p == 1)
     def _():
         sent(0)
 
-    @pl.when(has_z_out)
+    @pl.when(c == 0)
     def _():
         sent(1)
 
+    @pl.when(odd_low)
+    def _():
+        sent(1, EARLY)
+        sent(5, 0, EARLY)
+
+    @pl.when(odd_high)
+    def _():
+        sent(6, 0, EARLY)
+
     @pl.when(c == 1)
     def _():
         sent(2)
 
     sent(3)
 
-    @pl.when(p == 0)
+    @pl.when((p + c) == 0)
+    def _():
+        sent(4, EARLY)
+
+    @pl.when(odd_low)
     def _():
         sent(4)
 
@@ -193,6 +215,17 @@
         def _():
             for step in range(1, col_count):
                 left_copy(t, step).wait_send()
+
+
+def write(chunks, width, held, out, sem):
+    def copy(j):
+        place = pl.ds(pl.multiple_of(j * width, width), width)
+        return pltpu.make_async_copy(held.at[j], out.at[:, place], sem.at[j])
+
+    for j in range(chunks):
+        copy(j).start()
+    for j in range(chunks):
+        copy(j).wait()
 
 
 def solution(mesh):
@@ -207,21 +240,27 @@
         dma = pltpu.SemaphoreType.DMA
         results = pl.pallas_call(
             functools.partial(kernel, grid_rows, col_count, width, start),
-            out_shape=[block] * 5,
+            out_shape=[pltpu.VMEM((chunks, rows, width), jnp.bfloat16)] + [block] * 4,
             in_specs=[pl.BlockSpec(memory_space=pl.ANY)] * 2,
-            out_specs=[pl.BlockSpec(memory_space=pl.ANY)] * 5,
+            out_specs=[pl.BlockSpec(memory_space=pltpu.VMEM)] + [pl.BlockSpec(memory_space=pl.ANY)] * 4,
             scratch_shapes=[
                 pltpu.VMEM((rows, STEPS * rows), jnp.bfloat16),
                 pltpu.VMEM((BURST, STEPS * rows, width), jnp.bfloat16),
-                pltpu.VMEM((BURST, rows, width), jnp.bfloat16),
                 dma((chunks,)), dma((chunks,)), dma((chunks,)), dma((chunks,)),
-                dma((5,)), dma((STEPS, col_count - 1)), dma((STEPS,)),
-                dma((BURST, STEPS)), dma((BURST,)),
+                dma((7,)), dma((STEPS, col_count - 1)), dma((STEPS,)),
+                dma((BURST, STEPS)),
             ],
             compiler_params=pltpu.CompilerParams(
-                collective_id=0, has_side_effects=True, vmem_limit_bytes=60 * 1024 * 1024),
+                collective_id=0, has_side_effects=True, vmem_limit_bytes=40 * 1024 * 1024),
         )(left, right)
-        return results[0]
+        return pl.pallas_call(
+            functools.partial(write, chunks, width),
+            out_shape=block,
+            in_specs=[pl.BlockSpec(memory_space=pltpu.VMEM)],
+            out_specs=pl.BlockSpec(memory_space=pl.ANY),
+            scratch_shapes=[dma((chunks,))],
+            compiler_params=pltpu.CompilerParams(vmem_limit_bytes=20 * 1024 * 1024),
+        )(results[0])
 
     return jax.shard_map(
         local,

time: 401 us -> 391 us (0.975)
  local copies, waits for them, and re-layouts: 14 us -> 0 us
  Pallas kernels: 380 us -> 385 us
    unnamed x1 -> x0, local copies, waits for them, and re-layouts: 14 us -> none
    pallas_call x0 -> x1, Pallas kernels: none -> 6.08 us  [local(): pl.pallas_call(functools.partial(write, chunks, width), out_shape=block,...]
where the time goes in v2:
time: 391 us; the launch traced here: 385 us
  Pallas kernels  385 us (98%)
    pallas_call x1, Pallas kernels, local(): pl.pallas_call(functools.partial(kernel, grid_rows, col_count, width, sta...  379 us

profile of v2, /device:TPU:0, one launch (start us, length us, event | category | flops | bytes accessed | tf_op | source)
XLA Modules:
  0.0 384.8 jit_solution(9775675916559115275)
XLA Ops:
  0.0 378.8 %shard_map.28 = (bf16[32,1024,256]{2,1,0:T(8,128)(2,1)S(1)}, bf16[1024,8192]{1,0:T(8,128)(2,1)}, bf16[1024,8192]{1,0:T(8,128)(2,1)}, bf16[1024,8192]{1,0:T(8,128)(2,1)}, bf16[1024,8192]{1,0:T(8,128)(2,1)}) custom-call(bf16[1024,8192]{1,0:T(8,128)(2,1)} %left.1, bf16[1024,8192]{1,0:T(8,128)(2,1)} %right.1), custom_call_target="tpu_custom_call" | custom-call | tf_op jit(solution)/shard_map/pallas_call | solution.py:241
  378.8 6.1 %shard_map.29 = bf16[1024,8192]{1,0:T(8,128)(2,1)} custom-call(bf16[32,1024,256]{2,1,0:T(8,128)(2,1)S(1)} %get-tuple-element.6.held), custom_call_target="tpu_custom_call" | custom-call | tf_op jit(solution)/shard_map/pallas_call | solution.py:256

commit v3 on v2

--- a/solution.py
+++ b/solution.py
@@ -15,8 +15,8 @@
 MESH = pl.DeviceIdType.MESH
 
 
-def kernel(grid_rows, col_count, width, start, left, right, out, arr_a, arr_b, arr_z, arr_d,
-           lbuf, rbuf, sem_a, sem_b, sem_z, sem_d, send, lsend, lrecv, load_sem):
+def kernel(grid_rows, col_count, width, start, left, right, out, lbuf, arr_a, arr_b, arr_z, arr_d,
+           rbuf, sem_a, sem_b, sem_z, sem_d, send, lsend, lrecv, load_sem):
     row = lax.axis_index("row")
     col = lax.axis_index("col")
     rows, columns = right.shape
@@ -49,7 +49,6 @@
         pltpu.make_async_copy(cut(dst, j), cut(dst, j), recv.at[j]).wait()
 
     has_z_out = (p * c) == 0
-    has_z_in = ((1 - p) + c) > 0
 
     odd_low = (1 - p) * c == 1
     odd_high = p * c == 1
@@ -111,13 +110,24 @@
             arrival(arr_d, sem_d, i)
             remote(arr_d, arr_a, i, 6, sem_a, z_to).start()
 
-        @pl.when(has_z_in & ((c == 1) | (i >= EARLY)))
-        def _():
-            arrival(arr_z, sem_z, i)
+        def relay_z(j):
+            arrival(arr_z, sem_z, j)
 
             @pl.when(p == 0)
             def _():
-                remote(arr_z, arr_a, i, 4, sem_a, across).start()
+                remote(arr_z, arr_a, j, 4, sem_a, across).start()
+
+        @pl.when(((p + c) == 0) & (i + EARLY < chunks))
+        def _():
+            relay_z(i + EARLY)
+
+        @pl.when((c == 1) & (i < chunks - 1))
+        def _():
+            relay_z(i)
+
+        @pl.when((c == 1) & (i == chunks - 2))
+        def _():
+            relay_z(i + 1)
 
         arrival(arr_a, sem_a, i)
         remote(arr_a, arr_b, i, 3, sem_b, partner).start()
@@ -173,7 +183,13 @@
         compute(i, 1)
         return 0
 
-    lax.fori_loop(caught, chunks, level, 0)
+    lax.fori_loop(caught, chunks - 1, level, 0)
+    relay(chunks - 1)
+    arrival(arr_b, sem_b, chunks - 1)
+
+    @pl.when(c == 0)
+    def _():
+        arrival(arr_d, sem_d, chunks - 1)
 
     def sent(which, begin=0, end=chunks):
         part = right.at[:, pl.ds(begin * width, (end - begin) * width)]
@@ -217,13 +233,37 @@
                 left_copy(t, step).wait_send()
 
 
-def write(chunks, width, held, out, sem):
+def write(chunks, width, held, lbuf, right, arr_a, arr_b, arr_z, arr_d, out, rbuf, obuf, sem, load_sem):
+    c = lax.axis_index("row") % 2
+    rows = right.shape[0]
+    last = chunks - 1
+
+    def load(src, t):
+        return pltpu.make_async_copy(
+            src.at[:, pl.ds(last * width, width)], rbuf.at[pl.ds(t * rows, rows), :], load_sem.at[t])
+
+    load(right, 0).start()
+    load(arr_a, 1).start()
+    load(arr_b, 2).start()
+
+    @pl.when(c == 0)
+    def _():
+        load(arr_d, 3).start()
+
+    @pl.when(c == 1)
+    def _():
+        load(arr_z, 3).start()
+
     def copy(j):
-        place = pl.ds(pl.multiple_of(j * width, width), width)
-        return pltpu.make_async_copy(held.at[j], out.at[:, place], sem.at[j])
-
-    for j in range(chunks):
+        src = obuf if j == last else held.at[j]
+        return pltpu.make_async_copy(src, out.at[:, pl.ds(j * width, width)], sem.at[j])
+
+    for j in range(last):
         copy(j).start()
+    for t in range(STEPS):
+        load(right, t).wait()
+    obuf[...] = jnp.dot(lbuf[...], rbuf[...], preferred_element_type=jnp.float32).astype(obuf.dtype)
+    copy(last).start()
     for j in range(chunks):
         copy(j).wait()
 
@@ -240,27 +280,33 @@
         dma = pltpu.SemaphoreType.DMA
         results = pl.pallas_call(
             functools.partial(kernel, grid_rows, col_count, width, start),
-            out_shape=[pltpu.VMEM((chunks, rows, width), jnp.bfloat16)] + [block] * 4,
+            out_shape=[
+                pltpu.VMEM((chunks - 1, rows, width), jnp.bfloat16),
+                pltpu.VMEM((rows, STEPS * rows), jnp.bfloat16),
+            ] + [block] * 4,
             in_specs=[pl.BlockSpec(memory_space=pl.ANY)] * 2,
-            out_specs=[pl.BlockSpec(memory_space=pltpu.VMEM)] + [pl.BlockSpec(memory_space=pl.ANY)] * 4,
+            out_specs=[pl.BlockSpec(memory_space=pltpu.VMEM)] * 2 + [pl.BlockSpec(memory_space=pl.ANY)] * 4,
             scratch_shapes=[
-                pltpu.VMEM((rows, STEPS * rows), jnp.bfloat16),
                 pltpu.VMEM((BURST, STEPS * rows, width), jnp.bfloat16),
                 dma((chunks,)), dma((chunks,)), dma((chunks,)), dma((chunks,)),
                 dma((7,)), dma((STEPS, col_count - 1)), dma((STEPS,)),
                 dma((BURST, STEPS)),
             ],
             compiler_params=pltpu.CompilerParams(
-                collective_id=0, has_side_effects=True, vmem_limit_bytes=40 * 1024 * 1024),
+                collective_id=0, has_side_effects=True, vmem_limit_bytes=30 * 1024 * 1024),
         )(left, right)
         return pl.pallas_call(
             functools.partial(write, chunks, width),
             out_shape=block,
-            in_specs=[pl.BlockSpec(memory_space=pltpu.VMEM)],
+            in_specs=[pl.BlockSpec(memory_space=pltpu.VMEM)] * 2 + [pl.BlockSpec(memory_space=pl.ANY)] * 5,
             out_specs=pl.BlockSpec(memory_space=pl.ANY),
-            scratch_shapes=[dma((chunks,))],
+            scratch_shapes=[
+                pltpu.VMEM((STEPS * rows, width), jnp.bfloat16),
+                pltpu.VMEM((rows, width), jnp.bfloat16),
+                dma((chunks,)), dma((STEPS,)),
+            ],
             compiler_params=pltpu.CompilerParams(vmem_limit_bytes=20 * 1024 * 1024),
-        )(results[0])
+        )(*results[:2], right, *results[2:])
 
     return jax.shard_map(
         local,

time: 391 us -> 389 us (level); the launches traced: 385 us -> 389 us
  local copies, waits for them, and re-layouts: 0 us -> 11.6 us
  Pallas kernels: 385 us -> 377 us
    unnamed x0 -> x4, local copies, waits for them, and re-layouts: none -> 11.6 us
    pallas_call x1, Pallas kernels: 379 us -> 371 us  [local(): pl.pallas_call(functools.partial(kernel, grid_rows, col_count, width, sta...]
where the time goes in v3:
time: 389 us
  Pallas kernels  377 us (97%)
  local copies, waits for them, and re-layouts  11.6 us (3%)
    pallas_call x1, Pallas kernels, local(): pl.pallas_call(functools.partial(kernel, grid_rows, col_count, width, sta...  371 us
    unnamed x4, local copies, waits for them, and re-layouts  11.6 us

profile of v3, /device:TPU:0, one launch (start us, length us, event | category | flops | bytes accessed | tf_op | source)
XLA Modules:
  0.0 388.9 jit_solution(16087697444147788731)
XLA Ops:
  0.0 370.7 %shard_map.28 = (bf16[31,1024,256]{2,1,0:T(8,128)(2,1)S(1)}, bf16[1024,4096]{1,0:T(8,128)(2,1)S(1)}, bf16[1024,8192]{1,0:T(8,128)(2,1)}, bf16[1024,8192]{1,0:T(8...) custom-call(bf16[1024,8192]{1,0:T(8,128)(2,1)} %left.1, bf16[1024,8192]{1,0:T(8,128)(2,1)} %right.3), custom_call_target="tpu_custom_call" | custom-call | tf_op jit(solution)/shard_map/pallas_call | solution.py:281
  370.7 0.0 copy-start
  370.7 6.0 %copy-done = bf16[31,1024,256]{2,1,0:T(8,128)(2,1)} copy-done((bf16[31,1024,256]{2,1,0:T(8,128)(2,1)}, bf16[31,1024,256]{2,1,0:T(8,128)(2,1)S(1)}, u32[]{:S(2)}) %copy-start) | copy-done | bytes 16252952
  376.7 0.0 copy-start.1
  376.7 5.6 %copy-done.1 = bf16[31,1024,256]{2,1,0:T(8,128)(2,1)S(1)} copy-done((bf16[31,1024,256]{2,1,0:T(8,128)(2,1)S(1)}, bf16[31,1024,256]{2,1,0:T(8,128)(2,1)}, u32[]{:S(2)}) %copy-start.1) | copy-done | bytes 16252952
  382.3 6.6 %shard_map.29 = bf16[1024,8192]{1,0:T(8,128)(2,1)} custom-call(bf16[31,1024,256]{2,1,0:T(8,128)(2,1)S(1)} %copy-done.1, bf16[1024,4096]{1,0:T(8,128)(2,1)S(1)} %get-tuple-element.12.lbuf, bf16[1024,8192]{1,0:T(8,128)(2,1)} %right.3, bf16[1024,8192]{1,0:T(8,128)(2,1)} %get-tuple-element.13.arr_a, bf16[1024,8192]{1,0:T(8,128)(2,1)} %get-tuple-element.14.arr_b, ...), custom_call_target="tpu_custom_call" | custom-call | tf_op jit(solution)/shard_map/pallas_call | solution.py:298
Async XLA Ops:
  370.7 6.0 %copy-start = (bf16[31,1024,256]{2,1,0:T(8,128)(2,1)}, bf16[31,1024,256]{2,1,0:T(8,128)(2,1)S(1)}, u32[]{:S(2)}) copy-start(bf16[31,1024,256]{2,1,0:T(8,128)(2,1)S(1)} %get-tuple-element.11.held) | copy-start | bytes 48758788
  376.7 5.6 %copy-start.1 = (bf16[31,1024,256]{2,1,0:T(8,128)(2,1)S(1)}, bf16[31,1024,256]{2,1,0:T(8,128)(2,1)}, u32[]{:S(2)}) copy-start(bf16[31,1024,256]{2,1,0:T(8,128)(2,1)} %copy-done) | copy-start | bytes 48758788
